TPU v7x, 32 devices: a whole 2x2x4 slice. The times are simulated.
32 devices in a mesh: mol: 2 (over x), pts: 16 (over z, y, core).
Axes of the slice: x: 2, y: 2, z: 4, core: 2. Of those that a mesh axis runs over, the one named last changes fastest.
Arguments:
- points_map: bfloat16 [12800, 800], P(('mol', 'pts')), parts along dimension 0, may hold values from -0.21875 to 0.21875
- trial: bfloat16 [12800, 128], P('mol'), parts along dimension 0, may hold values from -6 to 6
- core: bfloat16 [12800, 6400], P(('mol', 'pts')), parts along dimension 0, may hold values from -2 to 4, as said below
- walkers: bfloat16 [1600, 12, 128], P('mol'), parts along dimension 0, may hold values from -6 to 6
- draws: int32 [12800, 12], P(('mol', 'pts')), parts along dimension 0, may hold values from 0 to 3
Outputs:
- new_walkers: bfloat16 [1600, 12, 128], P(('mol', 'pts')), parts along dimension 0
- energy: float32 [24], P('mol'), parts along dimension 0
There are 2 independent parts, one for each index of `mol`. A program takes and returns all parts, laid end to end along the dimension named above; each array names one. Nothing has to cross between parts.
Inputs may be any that keep to these rules, and one draw needn't show every extreme that they name: core is symmetric.
All inputs are finite; a program needn't handle non-finite values.
Results may differ from a plain program's by a relative error of at most 0.018.
Values may be sent and summed in bfloat16 or wider, within the bound.
A program may use at most 192 MiB of HBM per device.

v0:
```python
import math

import jax
import jax.numpy as jnp
from jax import lax
from jax.sharding import PartitionSpec as P

TAYLOR = 3


GAUSS_NODES = (-2.3344142, -0.7419637, 0.7419637, 2.3344142)
FIELD_STEP = 0.15


def node_lookup(draws):
    values = jnp.zeros(draws.shape, jnp.float32)
    for number, node in enumerate(GAUSS_NODES):
        values = values + jnp.where(draws == number, node, 0.0).astype(jnp.float32)
    return values


def body(points_map, trial, core, walkers, draws):
    point_rows = points_map.shape[0]
    orbitals = points_map.shape[1]
    walker_count = walkers.shape[1]
    occupied = walkers.shape[2]
    point_first = lax.axis_index("pts") * point_rows
    trial_here = lax.dynamic_slice_in_dim(trial, point_first, point_rows, 0)
    flat_walkers = walkers.reshape(orbitals, walker_count * occupied)
    orbit = (
        jnp.dot(points_map, flat_walkers, preferred_element_type=jnp.float32)
        .astype(jnp.bfloat16)
        .reshape(point_rows, walker_count, occupied)
    )
    density = (
        jnp.sum(orbit.astype(jnp.float32) * trial_here.astype(jnp.float32)[:, None, :], axis=2)
        / math.sqrt(occupied)
    ).astype(jnp.bfloat16)
    core_block = core
    potential = jnp.dot(
        core_block,
        lax.all_gather(density, "pts", axis=0, tiled=True),
        preferred_element_type=jnp.float32,
    )
    field = FIELD_STEP * (node_lookup(draws) - FIELD_STEP * potential)
    local_walkers = jnp.moveaxis(orbit, 1, 0)
    core_block = core.astype(jnp.float32)

    def per_walker(operands):
        left_orb, right_orb = operands
        forward = jnp.dot(left_orb, trial.T, preferred_element_type=jnp.float32)
        backward = jnp.dot(trial_here, right_orb.T, preferred_element_type=jnp.float32)
        return jnp.sum(core_block * forward * backward)

    exchange = (
        lax.map(
            per_walker,
            (local_walkers, jnp.moveaxis(lax.all_gather(orbit, "pts", axis=0, tiled=True), 1, 0)),
        )
        / occupied
    )
    hartree = jnp.sum(density.astype(jnp.float32) * potential, axis=0)
    total_points = point_rows * lax.axis_size("pts")
    energy = lax.psum((hartree - exchange) / (2.0 * total_points), "pts")
    own_rows = orbitals // lax.axis_size("pts")
    map_full = lax.all_gather(points_map, "pts", axis=0, tiled=True)
    field_full = lax.all_gather(field, "pts", axis=0, tiled=True)
    own_cols = walker_count * occupied // lax.axis_size("pts")
    col_start = lax.axis_index("pts") * own_cols
    cols_walkers = lax.dynamic_slice_in_dim(flat_walkers, col_start, own_cols, 1)
    walker_ids = (col_start + jnp.arange(own_cols, dtype=jnp.int32)) // occupied
    field_cols = jnp.take(field_full, walker_ids, axis=1)
    running_cols = cols_walkers.astype(jnp.float32)
    term_cols = cols_walkers
    for degree in range(1, TAYLOR + 1):
        current_cols = jnp.dot(map_full, term_cols, preferred_element_type=jnp.float32).astype(
            jnp.bfloat16
        )
        scaled_cols = (field_cols * current_cols.astype(jnp.float32)).astype(jnp.bfloat16)
        summed_cols = jnp.einsum(
            "pi,pc->ic", map_full, scaled_cols, preferred_element_type=jnp.float32
        )
        term_cols = (summed_cols / degree).astype(jnp.bfloat16)
        running_cols = running_cols + term_cols.astype(jnp.float32)
    placed = lax.all_to_all(
        running_cols.astype(jnp.bfloat16), "pts", split_axis=0, concat_axis=1, tiled=True
    )
    return (placed.reshape(own_rows, walker_count, occupied), energy)


def solution(mesh):
    placed = (
        P(("mol", "pts"), None),
        P("mol", None),
        P(("mol", "pts"), None),
        P("mol", None, None),
        P(("mol", "pts"), None),
    )
    return jax.shard_map(
        body,
        mesh=mesh,
        in_specs=placed,
        out_specs=(P(("mol", "pts"), None, None), P("mol")),
        check_vma=False,
    )
```

profile of v0, /device:TPU:0, one launch (start us, length us, event | category | flops | bytes accessed | tf_op | source)
XLA Modules:
  0.0 381.3 jit_solution(17466998609298275406)
XLA Ops:
  8.0 4.5 %copy.18 = bf16[800,12,128]{0,2,1:T(8,128)(2,1)} copy(bf16[800,12,128]{2,0,1:T(8,128)(2,1)} %param.10) | data formatting | bytes 4915200 | tf_op args[3]
  12.5 3.3 convolution_convert_fusion.3
  15.7 1.2 copy_bitcast_fusion
  17.0 0.9 reshape.85
  17.9 1.1 fusion.32
  19.0 0.9 multiply_reduce_fusion
  20.1 25.9 %all-gather = bf16[16,400,12]{1,2,0:T(8,128)(2,1)S(1)} all-gather(bf16[1,400,12]{1,2,0:T(8,128)(2,1)S(1)} %fusion.25), channel_id=1, replica_groups=mesh['mol'=2,'pts'=16] {'pts'}, dimensions={0}, use_global_device_ids=true | all-gather | bytes 163200 | tf_op jit(solution)/shard_map/all_gather | solution.py:42
  46.4 4.0 %multiply_reduce_fusion.1 = (f32[12]{0:T(128)S(1)}, f32[1,400,12]{1,2,0:T(8,128)S(1)}) fusion(f32[400,12]{0,1:T(8,128)S(1)} %copy.19, s32[400,12]{0,1:T(8,128)S(1)} %copy-done.4, bf16[6400,12]{0,1:T(8,128)(2,1)S(1)} %reshape.96, bf16[400,6400]{1,0:T(8,128)(2,1)} %param.9), kind=kOutput, calls=%fused_computation.39 | convolution fusion | flops 61531188 | bytes 5331248 | tf_op jit(solution)/shard_map/dot_general | solution.py:40
  50.4 21.2 %all-gather.1 = f32[16,400,12]{1,2,0:T(8,128)S(1)} all-gather(f32[1,400,12]{1,2,0:T(8,128)S(1)} %get-tuple-element.75), channel_id=1, replica_groups=mesh['mol'=2,'pts'=16] {'pts'}, dimensions={0}, use_global_device_ids=true | all-gather | bytes 326400 | tf_op jit(solution)/shard_map/all_gather | solution.py:67
  72.1 1.5 gather_fusion
  73.6 36.2 %all-gather.5.cloned.1.call-done = bf16[6400,800]{1,0:T(8,128)(2,1)} async-done(((bf16[400,800]{1,0:T(8,128)(2,1)}), bf16[6400,800]{1,0:T(8,128)(2,1)}) %all-gather.5.cloned.1.call-update) | async-done | bytes 10240016 | tf_op jit(solution)/shard_map/all_gather | solution.py:66
  109.8 13.0 %convolution_convert_fusion.4 = bf16[96,800]{1,0:T(8,128)(2,1)S(1)} fusion(bf16[6400,800]{1,0:T(8,128)(2,1)} %all-gather.5.cloned.1.call-done, f32[96,6400]{1,0:T(8,128)S(1)} %gather_fusion, pred[96]{0:T(512)(128)(4,1)S(1)} %compare_and_fusion, bf16[800,1536]{0,1:T(8,128)(2,1)} %bitcast.74, s32[]{:T(128)S(6)} %select_n.54), kind=kOutput, calls=%fused_computation.28 | convolution fusion | flops 1969228800 | bytes 25720932 | tf_op jit(solution)/shard_map/pi,pc->ic/dot_general | solution.py:80
  122.9 13.4 %fusion.17 = bf16[96,800]{1,0:T(8,128)(2,1)S(1)} fusion(bf16[6400,800]{1,0:T(8,128)(2,1)} %all-gather.5.cloned.1.call-done, bf16[96,800]{1,0:T(8,128)(2,1)S(1)} %convolution_convert_fusion.4, f32[96,6400]{1,0:T(8,128)S(1)} %gather_fusion, pred[96]{0:T(512)(128)(4,1)S(1)} %compare_and_fusion), kind=kOutput, calls=%fused_computation.29 | convolution fusion | flops 1969305600 | bytes 13004896 | tf_op jit(solution)/shard_map/pi,pc->ic/dot_general | solution.py:80
  136.2 13.6 %fusion.22 = bf16[800,96]{0,1:T(8,128)(2,1)S(1)} fusion(bf16[6400,800]{1,0:T(8,128)(2,1)} %all-gather.5.cloned.1.call-done, bf16[96,800]{1,0:T(8,128)(2,1)S(1)} %fusion.17, f32[96,6400]{1,0:T(8,128)S(1)} %gather_fusion, pred[96]{0:T(512)(128)(4,1)S(1)} %compare_and_fusion, bf16[96,800]{1,0:T(8,128)(2,1)S(1)} %convolution_convert_fusion.4, ...), kind=kOutput, calls=%fused_computation.34 | convolution fusion | flops 1969920000 | bytes 26237444 | tf_op jit(solution)/shard_map/pi,pc->ic/dot_general | solution.py:80
  150.0 0.8 all_to_all.12
  150.8 4.7 %all-to-all-start = ((bf16[16,50,96]{2,1,0:T(8,128)(2,1)}), bf16[16,50,96]{2,1,0:T(8,128)(2,1)S(1)}, u32[]{:S(2)}, u32[]{:S(2)}) async-start(bf16[16,50,96]{2,1,0:T(8,128)(2,1)} %all_to_all.12), calls=%async_computation | async-start | bytes 458752 | tf_op jit(solution)/shard_map/all_to_all | solution.py:85
  155.5 7.2 %convert_element_type.121 = f32[400,6400]{1,0:T(8,128)} convert(bf16[400,6400]{1,0:T(8,128)(2,1)} %param.9) | non-fusion elementwise | flops 2560000 | bytes 15360000 | tf_op jit(solution)/shard_map/convert_element_type | solution.py:47
  162.7 1.3 copy.25
  164.0 5.1 %all-to-all-done = bf16[16,50,96]{2,1,0:T(8,128)(2,1)S(1)} async-done(((bf16[16,50,96]{2,1,0:T(8,128)(2,1)}), bf16[16,50,96]{2,1,0:T(8,128)(2,1)S(1)}, u32[]{:S(2)}, u32[]{:S(2)}) %all-to-all-start) | async-done | bytes 153632 | tf_op jit(solution)/shard_map/all_to_all | solution.py:85
  169.3 48.3 %all-gather.7.cloned.1.call-done = bf16[6400,12,128]{2,0,1:T(8,128)(2,1)} async-done(((bf16[400,12,128]{2,0,1:T(8,128)(2,1)}), bf16[6400,12,128]{2,0,1:T(8,128)(2,1)}) %all-gather.7.cloned.1.call-update) | async-done | bytes 19660816 | tf_op jit(solution)/shard_map/all_gather | solution.py:58
  217.6 123.1 %while.10 = (s32[]{:T(128)}, f32[12]{0:T(128)S(1)}, bf16[12,400,128]{2,1,0:T(8,128)(2,1)}, bf16[6400,128]{1,0:T(8,128)(2,1)}, f32[400,6400]{1,0:T(8,128)}, /*ind...) while((s32[]{:T(128)}, f32[12]{0:T(128)S(1)}, bf16[12,400,128]{2,1,0:T(8,128)(2,1)}, ...), condition=%wide.region_4.5_spmd, body=%wide.region_2.4_spmd.sunk | while | flops 1318400000 | bytes 75162760 | solution.py:56
  217.6 3.1 convolution_bitcast_fusion.3
  220.7 1.3 copy-done
  222.0 5.1 %fusion.57 = f32[]{:T(128)} fusion(f32[400,6400]{1,0:T(8,128)S(1)} %convolution_bitcast_fusion.3, f32[400,6400]{1,0:T(8,128)S(1)} %copy-done, bf16[6400,128]{1,0:T(8,128)(2,1)} %get-tuple-element.138, bf16[12,400,128]{2,1,0:T(8,128)(2,1)} %get-tuple-element.137, s32[]{:T(128)} %get-tuple-element.127), kind=kOutput, calls=%fused_computation.4.clone.1 | convolution fusion | flops 663040000 | bytes 22221316 | tf_op jit(solution)/shard_map/while/body/eval_jaxpr/dot_general | solution.py:51
  227.1 0.8 dynamic_update_slice.5
  227.9 3.1 convolution_bitcast_fusion.3
  230.9 1.3 copy-done
  232.3 5.1 %fusion.57 = f32[]{:T(128)} fusion(f32[400,6400]{1,0:T(8,128)S(1)} %convolution_bitcast_fusion.3, f32[400,6400]{1,0:T(8,128)S(1)} %copy-done, bf16[6400,128]{1,0:T(8,128)(2,1)} %get-tuple-element.138, bf16[12,400,128]{2,1,0:T(8,128)(2,1)} %get-tuple-element.137, s32[]{:T(128)} %get-tuple-element.127), kind=kOutput, calls=%fused_computation.4.clone.1 | convolution fusion | flops 663040000 | bytes 22221316 | tf_op jit(solution)/shard_map/while/body/eval_jaxpr/dot_general | solution.py:51
  238.1 3.1 convolution_bitcast_fusion.3
  241.2 1.3 copy-done
  242.5 5.1 %fusion.57 = f32[]{:T(128)} fusion(f32[400,6400]{1,0:T(8,128)S(1)} %convolution_bitcast_fusion.3, f32[400,6400]{1,0:T(8,128)S(1)} %copy-done, bf16[6400,128]{1,0:T(8,128)(2,1)} %get-tuple-element.138, bf16[12,400,128]{2,1,0:T(8,128)(2,1)} %get-tuple-element.137, s32[]{:T(128)} %get-tuple-element.127), kind=kOutput, calls=%fused_computation.4.clone.1 | convolution fusion | flops 663040000 | bytes 22221316 | tf_op jit(solution)/shard_map/while/body/eval_jaxpr/dot_general | solution.py:51
  248.4 3.1 convolution_bitcast_fusion.3
  251.5 1.3 copy-done
  252.8 5.1 %fusion.57 = f32[]{:T(128)} fusion(f32[400,6400]{1,0:T(8,128)S(1)} %convolution_bitcast_fusion.3, f32[400,6400]{1,0:T(8,128)S(1)} %copy-done, bf16[6400,128]{1,0:T(8,128)(2,1)} %get-tuple-element.138, bf16[12,400,128]{2,1,0:T(8,128)(2,1)} %get-tuple-element.137, s32[]{:T(128)} %get-tuple-element.127), kind=kOutput, calls=%fused_computation.4.clone.1 | convolution fusion | flops 663040000 | bytes 22221316 | tf_op jit(solution)/shard_map/while/body/eval_jaxpr/dot_general | solution.py:51
  258.6 3.1 convolution_bitcast_fusion.3
  261.7 1.3 copy-done
  263.0 5.1 %fusion.57 = f32[]{:T(128)} fusion(f32[400,6400]{1,0:T(8,128)S(1)} %convolution_bitcast_fusion.3, f32[400,6400]{1,0:T(8,128)S(1)} %copy-done, bf16[6400,128]{1,0:T(8,128)(2,1)} %get-tuple-element.138, bf16[12,400,128]{2,1,0:T(8,128)(2,1)} %get-tuple-element.137, s32[]{:T(128)} %get-tuple-element.127), kind=kOutput, calls=%fused_computation.4.clone.1 | convolution fusion | flops 663040000 | bytes 22221316 | tf_op jit(solution)/shard_map/while/body/eval_jaxpr/dot_general | solution.py:51
  268.9 3.1 convolution_bitcast_fusion.3
  272.0 1.3 copy-done
  273.3 5.1 %fusion.57 = f32[]{:T(128)} fusion(f32[400,6400]{1,0:T(8,128)S(1)} %convolution_bitcast_fusion.3, f32[400,6400]{1,0:T(8,128)S(1)} %copy-done, bf16[6400,128]{1,0:T(8,128)(2,1)} %get-tuple-element.138, bf16[12,400,128]{2,1,0:T(8,128)(2,1)} %get-tuple-element.137, s32[]{:T(128)} %get-tuple-element.127), kind=kOutput, calls=%fused_computation.4.clone.1 | convolution fusion | flops 663040000 | bytes 22221316 | tf_op jit(solution)/shard_map/while/body/eval_jaxpr/dot_general | solution.py:51
  278.4 0.8 dynamic_update_slice.5
  279.1 3.1 convolution_bitcast_fusion.3
  282.2 1.3 copy-done
  283.5 5.1 %fusion.57 = f32[]{:T(128)} fusion(f32[400,6400]{1,0:T(8,128)S(1)} %convolution_bitcast_fusion.3, f32[400,6400]{1,0:T(8,128)S(1)} %copy-done, bf16[6400,128]{1,0:T(8,128)(2,1)} %get-tuple-element.138, bf16[12,400,128]{2,1,0:T(8,128)(2,1)} %get-tuple-element.137, s32[]{:T(128)} %get-tuple-element.127), kind=kOutput, calls=%fused_computation.4.clone.1 | convolution fusion | flops 663040000 | bytes 22221316 | tf_op jit(solution)/shard_map/while/body/eval_jaxpr/dot_general | solution.py:51
  288.6 0.8 dynamic_update_slice.5
  289.4 3.1 convolution_bitcast_fusion.3
  292.5 1.3 copy-done
  293.8 5.1 %fusion.57 = f32[]{:T(128)} fusion(f32[400,6400]{1,0:T(8,128)S(1)} %convolution_bitcast_fusion.3, f32[400,6400]{1,0:T(8,128)S(1)} %copy-done, bf16[6400,128]{1,0:T(8,128)(2,1)} %get-tuple-element.138, bf16[12,400,128]{2,1,0:T(8,128)(2,1)} %get-tuple-element.137, s32[]{:T(128)} %get-tuple-element.127), kind=kOutput, calls=%fused_computation.4.clone.1 | convolution fusion | flops 663040000 | bytes 22221316 | tf_op jit(solution)/shard_map/while/body/eval_jaxpr/dot_general | solution.py:51
  298.9 0.8 dynamic_update_slice.5
  299.7 3.1 convolution_bitcast_fusion.3
  302.7 1.3 copy-done
  304.1 5.1 %fusion.57 = f32[]{:T(128)} fusion(f32[400,6400]{1,0:T(8,128)S(1)} %convolution_bitcast_fusion.3, f32[400,6400]{1,0:T(8,128)S(1)} %copy-done, bf16[6400,128]{1,0:T(8,128)(2,1)} %get-tuple-element.138, bf16[12,400,128]{2,1,0:T(8,128)(2,1)} %get-tuple-element.137, s32[]{:T(128)} %get-tuple-element.127), kind=kOutput, calls=%fused_computation.4.clone.1 | convolution fusion | flops 663040000 | bytes 22221316 | tf_op jit(solution)/shard_map/while/body/eval_jaxpr/dot_general | solution.py:51
  309.2 0.8 dynamic_update_slice.5
  309.9 3.1 convolution_bitcast_fusion.3
  313.0 1.3 copy-done
  314.3 5.1 %fusion.57 = f32[]{:T(128)} fusion(f32[400,6400]{1,0:T(8,128)S(1)} %convolution_bitcast_fusion.3, f32[400,6400]{1,0:T(8,128)S(1)} %copy-done, bf16[6400,128]{1,0:T(8,128)(2,1)} %get-tuple-element.138, bf16[12,400,128]{2,1,0:T(8,128)(2,1)} %get-tuple-element.137, s32[]{:T(128)} %get-tuple-element.127), kind=kOutput, calls=%fused_computation.4.clone.1 | convolution fusion | flops 663040000 | bytes 22221316 | tf_op jit(solution)/shard_map/while/body/eval_jaxpr/dot_general | solution.py:51
  319.4 0.8 dynamic_update_slice.5
  320.2 3.1 convolution_bitcast_fusion.3
  323.3 1.3 copy-done
  324.6 5.1 %fusion.57 = f32[]{:T(128)} fusion(f32[400,6400]{1,0:T(8,128)S(1)} %convolution_bitcast_fusion.3, f32[400,6400]{1,0:T(8,128)S(1)} %copy-done, bf16[6400,128]{1,0:T(8,128)(2,1)} %get-tuple-element.138, bf16[12,400,128]{2,1,0:T(8,128)(2,1)} %get-tuple-element.137, s32[]{:T(128)} %get-tuple-element.127), kind=kOutput, calls=%fused_computation.4.clone.1 | convolution fusion | flops 663040000 | bytes 22221316 | tf_op jit(solution)/shard_map/while/body/eval_jaxpr/dot_general | solution.py:51
  330.4 3.1 convolution_bitcast_fusion.3
  333.5 1.3 copy-done
  334.8 5.1 %fusion.57 = f32[]{:T(128)} fusion(f32[400,6400]{1,0:T(8,128)S(1)} %convolution_bitcast_fusion.3, f32[400,6400]{1,0:T(8,128)S(1)} %copy-done, bf16[6400,128]{1,0:T(8,128)(2,1)} %get-tuple-element.138, bf16[12,400,128]{2,1,0:T(8,128)(2,1)} %get-tuple-element.137, s32[]{:T(128)} %get-tuple-element.127), kind=kOutput, calls=%fused_computation.4.clone.1 | convolution fusion | flops 663040000 | bytes 22221316 | tf_op jit(solution)/shard_map/while/body/eval_jaxpr/dot_general | solution.py:51
  341.4 33.1 %psum.7 = f32[12]{0:T(128)} all-reduce(f32[12]{0:T(128)S(1)} %subtract_multiply_fusion), channel_id=1, replica_groups=mesh['mol'=2,'pts'=16] {'pts'}, use_global_device_ids=true, to_apply=%region_5.6 | all-reduce | flops 12 | bytes 96 | tf_op jit(solution)/shard_map/psum | solution.py:64
  (45 shorter events, 7.5 us)
Async XLA Ops:
  7.2 102.7 %all-gather.5.cloned.1.call-start = ((), (), s32[]{:S(2)}) async-start(), calls=%async_computation.1 | async-start | bytes 12185600 | tf_op jit(solution)/shard_map/all_gather | solution.py:66
  7.9 4.6 %copy-start.3 = (bf16[400,800]{1,0:T(8,128)(2,1)S(1)}, bf16[400,800]{1,0:T(8,128)(2,1)}, u32[]{:S(2)}) copy-start(bf16[400,800]{1,0:T(8,128)(2,1)} %param.7) | copy-start | bytes 1920004
  7.9 209.7 %all-gather.7.cloned.1.call-start = ((), (), s32[]{:S(2)}) async-start(), calls=%async_computation.2 | async-start | bytes 20889600 | tf_op jit(solution)/shard_map/all_gather | solution.py:58
  17.9 32.5 %copy-start.1 = (bf16[400,12,128]{2,1,0:T(8,128)(2,1)}, bf16[400,12,128]{2,1,0:T(8,128)(2,1)S(1)}, u32[]{:S(2)}) copy-start(bf16[400,12,128]{2,1,0:T(8,128)(2,1)S(1)} %reshape.85) | copy-start | bytes 3686404
  17.9 28.4 %copy-start.4 = (s32[400,12]{0,1:T(8,128)S(1)}, s32[400,12]{0,1:T(8,128)}, u32[]{:S(2)}) copy-start(s32[400,12]{0,1:T(8,128)} %param.11) | copy-start | bytes 57604
  150.8 18.3 %all-to-all-start = ((bf16[16,50,96]{2,1,0:T(8,128)(2,1)}), bf16[16,50,96]{2,1,0:T(8,128)(2,1)S(1)}, u32[]{:S(2)}, u32[]{:S(2)}) async-start(bf16[16,50,96]{2,1,0:T(8,128)(2,1)} %all_to_all.12), calls=%async_computation | async-start | bytes 458752 | tf_op jit(solution)/shard_map/all_to_all | solution.py:85
  155.5 7.2 %copy-start.2 = (bf16[400,12,128]{2,1,0:T(8,128)(2,1)S(1)}, bf16[400,12,128]{2,1,0:T(8,128)(2,1)}, u32[]{:S(2)}) copy-start(bf16[400,12,128]{2,1,0:T(8,128)(2,1)} %copy-done.1) | copy-start | bytes 3686404
  217.6 4.4 %copy-start = (f32[400,6400]{1,0:T(8,128)S(1)}, f32[400,6400]{1,0:T(8,128)}, u32[]{:S(2)}) copy-start(f32[400,6400]{1,0:T(8,128)} %get-tuple-element.139) | copy-start | bytes 30720004 | tf_op jit(solution)/shard_map/while
  227.9 4.4 %copy-start = (f32[400,6400]{1,0:T(8,128)S(1)}, f32[400,6400]{1,0:T(8,128)}, u32[]{:S(2)}) copy-start(f32[400,6400]{1,0:T(8,128)} %get-tuple-element.139) | copy-start | bytes 30720004 | tf_op jit(solution)/shard_map/while
  238.1 4.4 %copy-start = (f32[400,6400]{1,0:T(8,128)S(1)}, f32[400,6400]{1,0:T(8,128)}, u32[]{:S(2)}) copy-start(f32[400,6400]{1,0:T(8,128)} %get-tuple-element.139) | copy-start | bytes 30720004 | tf_op jit(solution)/shard_map/while
  248.4 4.4 %copy-start = (f32[400,6400]{1,0:T(8,128)S(1)}, f32[400,6400]{1,0:T(8,128)}, u32[]{:S(2)}) copy-start(f32[400,6400]{1,0:T(8,128)} %get-tuple-element.139) | copy-start | bytes 30720004 | tf_op jit(solution)/shard_map/while
  258.6 4.4 %copy-start = (f32[400,6400]{1,0:T(8,128)S(1)}, f32[400,6400]{1,0:T(8,128)}, u32[]{:S(2)}) copy-start(f32[400,6400]{1,0:T(8,128)} %get-tuple-element.139) | copy-start | bytes 30720004 | tf_op jit(solution)/shard_map/while
  268.9 4.4 %copy-start = (f32[400,6400]{1,0:T(8,128)S(1)}, f32[400,6400]{1,0:T(8,128)}, u32[]{:S(2)}) copy-start(f32[400,6400]{1,0:T(8,128)} %get-tuple-element.139) | copy-start | bytes 30720004 | tf_op jit(solution)/shard_map/while
  279.1 4.4 %copy-start = (f32[400,6400]{1,0:T(8,128)S(1)}, f32[400,6400]{1,0:T(8,128)}, u32[]{:S(2)}) copy-start(f32[400,6400]{1,0:T(8,128)} %get-tuple-element.139) | copy-start | bytes 30720004 | tf_op jit(solution)/shard_map/while
  289.4 4.4 %copy-start = (f32[400,6400]{1,0:T(8,128)S(1)}, f32[400,6400]{1,0:T(8,128)}, u32[]{:S(2)}) copy-start(f32[400,6400]{1,0:T(8,128)} %get-tuple-element.139) | copy-start | bytes 30720004 | tf_op jit(solution)/shard_map/while
  299.7 4.4 %copy-start = (f32[400,6400]{1,0:T(8,128)S(1)}, f32[400,6400]{1,0:T(8,128)}, u32[]{:S(2)}) copy-start(f32[400,6400]{1,0:T(8,128)} %get-tuple-element.139) | copy-start | bytes 30720004 | tf_op jit(solution)/shard_map/while
  309.9 4.4 %copy-start = (f32[400,6400]{1,0:T(8,128)S(1)}, f32[400,6400]{1,0:T(8,128)}, u32[]{:S(2)}) copy-start(f32[400,6400]{1,0:T(8,128)} %get-tuple-element.139) | copy-start | bytes 30720004 | tf_op jit(solution)/shard_map/while
  320.2 4.4 %copy-start = (f32[400,6400]{1,0:T(8,128)S(1)}, f32[400,6400]{1,0:T(8,128)}, u32[]{:S(2)}) copy-start(f32[400,6400]{1,0:T(8,128)} %get-tuple-element.139) | copy-start | bytes 30720004 | tf_op jit(solution)/shard_map/while
  330.4 4.4 %copy-start = (f32[400,6400]{1,0:T(8,128)S(1)}, f32[400,6400]{1,0:T(8,128)}, u32[]{:S(2)}) copy-start(f32[400,6400]{1,0:T(8,128)} %get-tuple-element.139) | copy-start | bytes 30720004 | tf_op jit(solution)/shard_map/while
Sparse Core Ops, SparseCore 0:
  10.1 99.6 all-gather.4
  111.4 106.1 all-gather.6
where the time goes:
time: 382 us; the launch traced here: 381 us
  matrix products  146 us (38%)
  waiting for transfers between devices  90.3 us (24%)
  blocking collectives  80.1 us (21%)
  local copies, waits for them, and re-layouts  37.2 us (10%)
  between operations  14.2 us (4%)
  other arithmetic  9.22 us (2%)
  starting transfers between devices  4.76 us (1%)
    dot_general x12, matrix products, per_walker(): forward = jnp.dot(left_orb, trial.T, preferred_element_type=jnp.float32)  61.2 us
    all_gather x1, waiting for transfers between devices, body(): lax.all_gather(orbit, 'pts', axis=0, tiled=True)  48.3 us
    dot_general x3, matrix products, body(): jnp.einsum('pi,pc->ic', map_full, scaled_cols, preferred_element_type=jnp...  40 us
    dot_general x12, matrix products, per_walker(): jnp.dot(trial_here, right_orb.T, preferred_element_type=jnp.float32)  37.1 us
    all_gather x1, waiting for transfers between devices, body(): map_full = lax.all_gather(points_map, 'pts', axis=0, tiled=True)  36.2 us
    psum x1, blocking collectives, body(): energy = lax.psum((hartree - exchange) / (2.0 * total_points), 'pts')  33.1 us
    all_gather x1, blocking collectives, body(): lax.all_gather(density, 'pts', axis=0, tiled=True)  25.9 us
    all_gather x1, blocking collectives, body(): field_full = lax.all_gather(field, 'pts', axis=0, tiled=True)  21.2 us
  transfers between devices with their start and end apart: 3, of which 3 were waited for; matrix products, arithmetic and copies ran while one was open for 18% of the time, Pallas kernels for 0%

commit v1 on v0

v1 whole, which is shorter than its diff:
```python
import functools
import math

import jax
import jax.numpy as jnp
from jax import lax
from jax.experimental import pallas as pl
from jax.experimental.pallas import tpu as pltpu
from jax.sharding import PartitionSpec as P

TAYLOR = 3


GAUSS_NODES = (-2.3344142, -0.7419637, 0.7419637, 2.3344142)
FIELD_STEP = 0.15
LANES = 128
CONTRACT_LAST = (((1,), (1,)), ((), ()))
CONTRACT_FIRST = (((0,), (0,)), ((), ()))


def node_lookup(draws):
    values = jnp.zeros(draws.shape, jnp.float32)
    for number, node in enumerate(GAUSS_NODES):
        values = values + jnp.where(draws == number, node, 0.0).astype(jnp.float32)
    return values


def dot(left, right, dims):
    return lax.dot_general(left, right, dims, preferred_element_type=jnp.float32)


def exchange_kernel(n, walker_count, map_ref, trial_ref, trial_own, core_ref, walkers_ref, orbit_own, out_ref, blocks):
    rows, occupied = trial_own.shape
    window = blocks.shape[0]
    step = pl.program_id(0)
    me = lax.axis_index("pts")
    block = lax.rem(me + step, n)
    first = block * rows
    base = pl.multiple_of(first // LANES * LANES, LANES)
    shift = pl.multiple_of(first - base, 16)

    @pl.when(step == 0)
    def _():
        out_ref[...] = jnp.zeros_like(out_ref)

    blocks[...] = jnp.zeros_like(blocks)
    weight = jnp.where(jnp.logical_or(step == 0, 2 * step == n), 1.0, 2.0)
    blocks[pl.ds(shift, rows), :] = dot(
        map_ref[0], walkers_ref[...], (((1,), (0,)), ((), ()))
    ).astype(jnp.bfloat16)
    core_here = core_ref[:, pl.ds(base, window)].astype(jnp.float32)
    trial_there = trial_ref[pl.ds(base, window), :]
    for walker in range(walker_count):
        cols = slice(walker * occupied, (walker + 1) * occupied)
        forward = dot(orbit_own[:, cols], trial_there, CONTRACT_LAST)
        backward = dot(trial_own[...], blocks[:, cols], CONTRACT_LAST)
        product = core_here * forward * backward
        out_ref[walker] += weight * jnp.sum(product.reshape(rows // 8, 8, window), axis=0)


def exchange_sums(n, walker_count, map_full, trial, trial_here, core, flat_walkers, orbit):
    rows, orbitals = map_full.shape[0] // n, map_full.shape[1]
    columns = flat_walkers.shape[1]
    window = (rows + (LANES - 16) + LANES - 1) // LANES * LANES
    steps = n // 2 + 1
    whole = lambda a: pl.BlockSpec(a.shape, lambda s: (0,) * a.ndim)
    flops = 2 * steps * (rows * orbitals * columns + 2 * rows * window * columns)
    return pl.pallas_call(
        functools.partial(exchange_kernel, n, walker_count),
        grid=(steps,),
        out_shape=jax.ShapeDtypeStruct((walker_count, 8, window), jnp.float32),
        in_specs=[
            pl.BlockSpec((1, rows, orbitals), lambda s: (lax.rem(lax.axis_index("pts") + s, n), 0, 0)),
            whole(trial),
            whole(trial_here),
            whole(core),
            whole(flat_walkers),
            whole(orbit),
        ],
        out_specs=pl.BlockSpec((walker_count, 8, window), lambda s: (0, 0, 0)),
        scratch_shapes=[pltpu.VMEM((window, columns), jnp.bfloat16)],
        cost_estimate=pl.CostEstimate(flops=flops, bytes_accessed=2 * map_full.size, transcendentals=0),
        compiler_params=pltpu.CompilerParams(vmem_limit_bytes=60 * 2**20),
        name="exchange",
    )(map_full.reshape(n, rows, orbitals), trial, trial_here, core, flat_walkers, orbit)


def propagate_kernel(n, occupied, piece, map_ref, field_ref, cols_ref, out_ref, wide, total, term):
    points, orbitals = map_ref.shape
    own = cols_ref.shape[0]
    start = lax.axis_index("pts") * own
    walker_ids = (start + lax.broadcasted_iota(jnp.int32, (1, own), 1)) // occupied
    low = start // occupied
    span = (own + occupied - 2) // occupied + 1
    running = cols_ref[...].astype(jnp.float32)
    term[...] = cols_ref[...]
    for degree in range(1, TAYLOR + 1):
        total[...] = jnp.zeros_like(total)

        @pl.loop(0, points // piece)
        def _(number):
            here = pl.ds(pl.multiple_of(number * piece, piece), piece)
            if degree == 1:
                field = field_ref[here, :]
                lane = lax.broadcasted_iota(jnp.int32, field.shape, 1)
                spread = jnp.zeros((piece, own), jnp.float32)
                for offset in range(span):
                    column = jnp.sum(jnp.where(lane == low + offset, field, 0.0), axis=1, keepdims=True)
                    spread = jnp.where(walker_ids == low + offset, column, spread)
                wide[here, :] = spread
            block = map_ref[here, :]
            current = dot(block, term[...], CONTRACT_LAST).astype(jnp.bfloat16)
            scaled = (wide[here, :] * current.astype(jnp.float32)).astype(jnp.bfloat16)
            total[...] += dot(scaled, block, CONTRACT_FIRST)

        term[...] = (total[...] / degree).astype(jnp.bfloat16)
        running = running + term[...].astype(jnp.float32)
    out_ref[...] = running.astype(jnp.bfloat16)


def propagate(n, occupied, map_full, field_full, own_cols_t):
    points, orbitals = map_full.shape
    own = own_cols_t.shape[0]
    piece = next(p for p in (1280, 640, 256, points // n) if points % p == 0)
    return pl.pallas_call(
        functools.partial(propagate_kernel, n, occupied, piece),
        out_shape=jax.ShapeDtypeStruct((own, orbitals), jnp.bfloat16),
        in_specs=[pl.BlockSpec(memory_space=pltpu.VMEM)] * 3,
        out_specs=pl.BlockSpec(memory_space=pltpu.VMEM),
        scratch_shapes=[
            pltpu.VMEM((points, own), jnp.float32),
            pltpu.VMEM((own, orbitals), jnp.float32),
            pltpu.VMEM((own, orbitals), jnp.bfloat16),
        ],
        cost_estimate=pl.CostEstimate(
            flops=12 * points * orbitals * own, bytes_accessed=2 * map_full.size, transcendentals=0
        ),
        compiler_params=pltpu.CompilerParams(vmem_limit_bytes=60 * 2**20),
        name="propagate",
    )(map_full, field_full, own_cols_t)


def exchange_plain(trial, trial_here, core, orbit):
    core_block = core.astype(jnp.float32)

    def per_walker(operands):
        left_orb, right_orb = operands
        forward = jnp.dot(left_orb, trial.T, preferred_element_type=jnp.float32)
        backward = jnp.dot(trial_here, right_orb.T, preferred_element_type=jnp.float32)
        return jnp.sum(core_block * forward * backward)

    everyone = lax.all_gather(orbit, "pts", axis=0, tiled=True)
    return lax.map(per_walker, (jnp.moveaxis(orbit, 1, 0), jnp.moveaxis(everyone, 1, 0)))


def body(points_map, trial, core, walkers, draws):
    point_rows = points_map.shape[0]
    orbitals = points_map.shape[1]
    walker_count = walkers.shape[1]
    occupied = walkers.shape[2]
    n = lax.axis_size("pts")
    map_full = lax.all_gather(points_map, "pts", axis=0, tiled=True)
    point_first = lax.axis_index("pts") * point_rows
    trial_here = lax.dynamic_slice_in_dim(trial, point_first, point_rows, 0)
    flat_walkers = walkers.reshape(orbitals, walker_count * occupied)
    flat_orbit = jnp.dot(points_map, flat_walkers, preferred_element_type=jnp.float32).astype(jnp.bfloat16)
    orbit = flat_orbit.reshape(point_rows, walker_count, occupied)
    density = (
        jnp.sum(orbit.astype(jnp.float32) * trial_here.astype(jnp.float32)[:, None, :], axis=2)
        / math.sqrt(occupied)
    ).astype(jnp.bfloat16)
    potential = jnp.dot(
        core,
        lax.all_gather(density, "pts", axis=0, tiled=True),
        preferred_element_type=jnp.float32,
    )
    field = FIELD_STEP * (node_lookup(draws) - FIELD_STEP * potential)
    field_full = lax.all_gather(field, "pts", axis=0, tiled=True)
    own_rows = orbitals // n
    own_cols = walker_count * occupied // n
    col_start = lax.axis_index("pts") * own_cols
    cols_walkers = lax.dynamic_slice_in_dim(flat_walkers, col_start, own_cols, 1)
    final_t = propagate(n, occupied, map_full, field_full, cols_walkers.T)
    placed = lax.all_to_all(final_t.T, "pts", split_axis=0, concat_axis=1, tiled=True)
    if point_rows % 16 == 0 and n % 2 == 0:
        exchange = jnp.sum(
            exchange_sums(n, walker_count, map_full, trial, trial_here, core, flat_walkers, flat_orbit),
            axis=(1, 2),
        )
    else:
        exchange = exchange_plain(trial, trial_here, core, orbit)
    hartree = jnp.sum(density.astype(jnp.float32) * potential, axis=0)
    total_points = point_rows * n
    energy = lax.psum((hartree - exchange / occupied) / (2.0 * total_points), "pts")
    return (placed.reshape(own_rows, walker_count, occupied), energy)


def solution(mesh):
    placed = (
        P(("mol", "pts"), None),
        P("mol", None),
        P(("mol", "pts"), None),
        P("mol", None, None),
        P(("mol", "pts"), None),
    )
    return jax.shard_map(
        body,
        mesh=mesh,
        in_specs=placed,
        out_specs=(P(("mol", "pts"), None, None), P("mol")),
        check_vma=False,
    )
```

time: 382 us -> 234 us (0.61)
  matrix products: 146 us -> 6.56 us
  Pallas kernels: 0 us -> 74.3 us
  waiting for transfers between devices: 90.3 us -> 32.8 us
  local copies, waits for them, and re-layouts: 37.2 us -> 15.7 us
  other arithmetic: 9.22 us -> 3.62 us
    dot_general x28 -> x1, matrix products: 142 us -> 4.03 us  [body(): jnp.dot(core, lax.all_gather(density, 'pts', axis=0, tiled=True), preferr...]
    pallas_call x0 -> x2, Pallas kernels: none -> 74.3 us  [the longest x1 42.2 us: exchange_sums(): pl.pallas_call(functools.partial(exchange_kernel, n, walker_count), grid=...]
    all_gather x1 -> x0, waiting for transfers between devices: 48.3 us -> none  [body(): lax.all_gather(orbit, 'pts', axis=0, tiled=True)]
    while x25 -> x0, local copies, waits for them, and re-layouts: 17.1 us -> none
    dynamic_update_slice x12 -> x0, local copies, waits for them, and re-layouts: 9.07 us -> none  [body(): lax.map(per_walker, (local_walkers, jnp.moveaxis(lax.all_gather(orbit, 'p...]
    convert_element_type x1 -> x0, other arithmetic: 7.18 us -> none  [body(): core_block = core.astype(jnp.float32)]
    all_to_all x1, waiting for transfers between devices: 5.06 us -> 0.01 us  [body(): lax.all_to_all(final_t.T, 'pts', split_axis=0, concat_axis=1, tiled=True)]
    all_gather x1, waiting for transfers between devices: 36.2 us -> 32.1 us  [body(): map_full = lax.all_gather(points_map, 'pts', axis=0, tiled=True)]
  transfers between devices with their start and end apart: 3 -> 2, of which waited for: 3 -> 1; matrix products, arithmetic and copies ran while one was open for 18% -> 10% of each run, Pallas kernels for 0% -> 18%
where the time goes in v1:
time: 234 us
  blocking collectives  82.3 us (35%)
  Pallas kernels  74.3 us (32%)
  waiting for transfers between devices  32.8 us (14%)
  local copies, waits for them, and re-layouts  15.7 us (7%)
  between operations  14.1 us (6%)
  matrix products  6.56 us (3%)
  starting transfers between devices  4.43 us (2%)
  other arithmetic  3.62 us (2%)
    pallas_call x1, Pallas kernels, exchange_sums(): pl.pallas_call(functools.partial(exchange_kernel, n, walker_count), grid=...  42.2 us
    psum x1, blocking collectives, body(): lax.psum((hartree - exchange / occupied) / (2.0 * total_points), 'pts')  34.3 us
    all_gather x1, waiting for transfers between devices, body(): map_full = lax.all_gather(points_map, 'pts', axis=0, tiled=True)  32.1 us
    pallas_call x1, Pallas kernels, propagate(): pl.pallas_call(functools.partial(propagate_kernel, n, occupied, piece), o...  32 us
    all_gather x1, blocking collectives, body(): lax.all_gather(density, 'pts', axis=0, tiled=True)  26 us
    all_gather x1, blocking collectives, body(): field_full = lax.all_gather(field, 'pts', axis=0, tiled=True)  22.1 us
  transfers between devices with their start and end apart: 2, of which 1 were waited for; matrix products, arithmetic and copies ran while one was open for 10% of the time, Pallas kernels for 18%

profile of v1, /device:TPU:0, one launch (start us, length us, event | category | flops | bytes accessed | tf_op | source)
XLA Modules:
  0.0 233.8 jit_solution(18420034898452729909)
XLA Ops:
  7.2 0.0 all-gather.4.cloned.1.call-start
  7.2 0.7 all-gather.4.cloned.1.call-update
  7.9 3.2 %copy.17 = bf16[800,12,128]{0,2,1:T(8,128)(2,1)S(1)} copy(bf16[800,12,128]{2,0,1:T(8,128)(2,1)} %param.8) | data formatting | bytes 4915200 | tf_op args[3]
  11.1 0.0 copy-start
  11.1 0.0 copy-start.1
  11.2 2.7 %copy.23.walkers_ref = bf16[800,1536]{1,0:T(8,128)(2,1)} copy(bf16[800,1536]{0,1:T(8,128)(2,1)S(1)} %bitcast.21) | data formatting | bytes 4915200 | tf_op jit(solution)/shard_map/reshape | solution.py:165
  13.9 0.0 copy-done
  13.9 0.0 copy-done.1
  13.9 2.5 %convolution_convert_fusion.orbit_own = bf16[400,1536]{1,0:T(8,128)(2,1)} fusion(bf16[400,800]{1,0:T(8,128)(2,1)S(1)} %copy-done.1, bf16[800,1536]{0,1:T(8,128)(2,1)S(1)} %bitcast.22), kind=kOutput, calls=%fused_computation.1 | convolution fusion | flops 983654400 | bytes 4326400 | tf_op jit(solution)/shard_map/dot_general | solution.py:166
  16.4 2.5 %reshape.24 = f32[400,12,128]{2,1,0:T(8,128)S(1)} reshape(bf16[400,1536]{1,0:T(8,128)(2,1)} %convolution_convert_fusion.orbit_own) | data formatting | bytes 3686400 | tf_op jit(solution)/shard_map/convert_element_type | solution.py:169
  18.9 0.0 copy-start.2
  18.9 1.6 fusion.1
  20.5 0.9 multiply_reduce_fusion
  21.4 0.1 copy.18
  21.5 26.0 %all-gather = bf16[16,400,12]{1,2,0:T(8,128)(2,1)S(1)} all-gather(bf16[1,400,12]{1,2,0:T(8,128)(2,1)S(1)} %fusion), channel_id=1, replica_groups=mesh['mol'=2,'pts'=16] {'pts'}, dimensions={0}, use_global_device_ids=true | all-gather | bytes 163200 | tf_op jit(solution)/shard_map/all_gather | solution.py:174
  47.5 0.1 copy.19
  47.6 0.3 reshape.26
  47.9 0.0 copy-done.2
  48.0 4.0 %multiply_reduce_fusion.1 = (f32[12]{0:T(128)S(1)}, f32[1,400,12]{1,2,0:T(8,128)S(1)}) fusion(f32[400,12]{0,1:T(8,128)S(1)} %copy.18, s32[400,12]{0,1:T(8,128)S(1)} %copy-done.2, bf16[6400,12]{0,1:T(8,128)(2,1)S(1)} %reshape.26, bf16[400,6400]{1,0:T(8,128)(2,1)} %core_ref.1), kind=kOutput, calls=%fused_computation.4 | convolution fusion | flops 61531188 | bytes 5331248 | tf_op jit(solution)/shard_map/dot_general | solution.py:172
  52.0 22.1 %all-gather.1 = f32[16,400,12]{1,2,0:T(8,128)S(1)} all-gather(f32[1,400,12]{1,2,0:T(8,128)S(1)} %get-tuple-element.9), channel_id=1, replica_groups=mesh['mol'=2,'pts'=16] {'pts'}, dimensions={0}, use_global_device_ids=true | all-gather | bytes 326400 | tf_op jit(solution)/shard_map/all_gather | solution.py:178
  74.1 2.4 %copy.20 = f32[16,400,12]{2,1,0:T(8,128)} copy(f32[16,400,12]{1,2,0:T(8,128)S(1)} %all-gather.1) | data formatting | bytes 614400 | tf_op jit(solution)/shard_map/all_gather | solution.py:178
  76.4 1.6 dynamic-slice_bitcast_fusion.cols_ref
  78.0 32.1 %all-gather.4.cloned.1.call-done.map_ref = bf16[6400,800]{1,0:T(8,128)(2,1)} async-done(((bf16[400,800]{1,0:T(8,128)(2,1)}), bf16[6400,800]{1,0:T(8,128)(2,1)}) %all-gather.4.cloned.1.call-update) | async-done | bytes 10240016 | tf_op jit(solution)/shard_map/all_gather | solution.py:162
  110.1 32.0 %propagate.1 = bf16[96,800]{1,0:T(8,128)(2,1)} custom-call(bf16[6400,800]{1,0:T(8,128)(2,1)} %all-gather.4.cloned.1.call-done.map_ref, f32[6400,12]{1,0:T(8,128)} %bitcast.24, bf16[96,800]{1,0:T(8,128)(2,1)} %dynamic-slice_bitcast_fusion.cols_ref), custom_call_target="tpu_custom_call" | custom-call | flops 5898240000 | bytes 10240000 | tf_op jit(solution)/shard_map/propagate/pallas_call | solution.py:125
  142.2 1.1 copy.21
  143.3 0.8 all_to_all.12
  144.0 4.4 %all-to-all-start = ((bf16[16,50,96]{2,1,0:T(8,128)(2,1)}), bf16[16,50,96]{2,1,0:T(8,128)(2,1)S(1)}, u32[]{:S(2)}, u32[]{:S(2)}) async-start(bf16[16,50,96]{2,1,0:T(8,128)(2,1)} %all_to_all.12), calls=%async_computation | async-start | bytes 458752 | tf_op jit(solution)/shard_map/all_to_all | solution.py:184
  148.4 42.2 %exchange.1 = f32[12,8,512]{2,1,0:T(8,128)} custom-call(bf16[16,400,800]{2,1,0:T(8,128)(2,1)} %bitcast.27, bf16[6400,128]{1,0:T(8,128)(2,1)} %trial_ref.1, bf16[400,128]{1,0:T(8,128)(2,1)} %get-tuple-element.7.trial_own, bf16[400,6400]{1,0:T(8,128)(2,1)} %core_ref.1, bf16[800,1536]{1,0:T(8,128)(2,1)} %copy.23.walkers_ref, ...), custom_call_target="tpu_custom_call" | custom-call | flops 20171980800 | bytes 10240000 | tf_op jit(solution)/shard_map/exchange/pallas_call | solution.py:68
  190.6 1.1 reduce_sum.29
  191.7 34.3 %psum.7 = f32[12]{0:T(128)} all-reduce(f32[12]{0:T(128)S(1)} %subtract_multiply_fusion), channel_id=1, replica_groups=mesh['mol'=2,'pts'=16] {'pts'}, use_global_device_ids=true, to_apply=%region_3.4 | all-reduce | flops 12 | bytes 96 | tf_op jit(solution)/shard_map/psum | solution.py:194
  226.1 0.0 all-to-all-done
  226.1 0.2 reshape.22
  226.3 0.7 copy.24
  (3 shorter events, 0.0 us)
Async XLA Ops:
  7.2 103.0 %all-gather.4.cloned.1.call-start = ((), (), s32[]{:S(2)}) async-start(), calls=%async_computation.1 | async-start | bytes 12185600 | tf_op jit(solution)/shard_map/all_gather | solution.py:162
  11.1 2.7 %copy-start = (bf16[800,12,128]{0,2,1:T(8,128)(2,1)}, bf16[800,12,128]{0,2,1:T(8,128)(2,1)S(1)}, u32[]{:S(2)}) copy-start(bf16[800,12,128]{0,2,1:T(8,128)(2,1)S(1)} %copy.17) | copy-start | bytes 7372804
  11.1 2.7 %copy-start.1 = (bf16[400,800]{1,0:T(8,128)(2,1)S(1)}, bf16[400,800]{1,0:T(8,128)(2,1)}, u32[]{:S(2)}) copy-start(bf16[400,800]{1,0:T(8,128)(2,1)} %param.5) | copy-start | bytes 1920004
  18.9 29.0 %copy-start.2 = (s32[400,12]{0,1:T(8,128)S(1)}, s32[400,12]{0,1:T(8,128)}, u32[]{:S(2)}) copy-start(s32[400,12]{0,1:T(8,128)} %param.9) | copy-start | bytes 57604
  144.0 82.0 %all-to-all-start = ((bf16[16,50,96]{2,1,0:T(8,128)(2,1)}), bf16[16,50,96]{2,1,0:T(8,128)(2,1)S(1)}, u32[]{:S(2)}, u32[]{:S(2)}) async-start(bf16[16,50,96]{2,1,0:T(8,128)(2,1)} %all_to_all.12), calls=%async_computation | async-start | bytes 458752 | tf_op jit(solution)/shard_map/all_to_all | solution.py:184
Sparse Core Ops, SparseCore 0:
  10.1 99.9 all-gather.3

commit v2 on v1

--- a/solution.py
+++ b/solution.py
@@ -29,28 +29,16 @@
     return lax.dot_general(left, right, dims, preferred_element_type=jnp.float32)
 
 
-def exchange_kernel(n, walker_count, map_ref, trial_ref, trial_own, core_ref, walkers_ref, orbit_own, out_ref, blocks):
+def add_exchange(out_ref, blocks, map_block, trial_ref, trial_own, core_ref, walkers_ref, orbit_own, first, weight):
     rows, occupied = trial_own.shape
     window = blocks.shape[0]
-    step = pl.program_id(0)
-    me = lax.axis_index("pts")
-    block = lax.rem(me + step, n)
-    first = block * rows
     base = pl.multiple_of(first // LANES * LANES, LANES)
     shift = pl.multiple_of(first - base, 16)
-
-    @pl.when(step == 0)
-    def _():
-        out_ref[...] = jnp.zeros_like(out_ref)
-
     blocks[...] = jnp.zeros_like(blocks)
-    weight = jnp.where(jnp.logical_or(step == 0, 2 * step == n), 1.0, 2.0)
-    blocks[pl.ds(shift, rows), :] = dot(
-        map_ref[0], walkers_ref[...], (((1,), (0,)), ((), ()))
-    ).astype(jnp.bfloat16)
+    blocks[pl.ds(shift, rows), :] = dot(map_block, walkers_ref[...], (((1,), (0,)), ((), ()))).astype(jnp.bfloat16)
     core_here = core_ref[:, pl.ds(base, window)].astype(jnp.float32)
     trial_there = trial_ref[pl.ds(base, window), :]
-    for walker in range(walker_count):
+    for walker in range(out_ref.shape[0]):
         cols = slice(walker * occupied, (walker + 1) * occupied)
         forward = dot(orbit_own[:, cols], trial_there, CONTRACT_LAST)
         backward = dot(trial_own[...], blocks[:, cols], CONTRACT_LAST)
@@ -58,31 +46,205 @@
         out_ref[walker] += weight * jnp.sum(product.reshape(rows // 8, 8, window), axis=0)
 
 
-def exchange_sums(n, walker_count, map_full, trial, trial_here, core, flat_walkers, orbit):
-    rows, orbitals = map_full.shape[0] // n, map_full.shape[1]
-    columns = flat_walkers.shape[1]
+def spread_field(field_ref, here, piece, start, own, occupied):
+    walker_ids = (start + lax.broadcasted_iota(jnp.int32, (1, own), 1)) // occupied
+    low = start // occupied
+    field = field_ref[here, :]
+    lane = lax.broadcasted_iota(jnp.int32, field.shape, 1)
+    spread = jnp.zeros((piece, own), jnp.float32)
+    for offset in range((own + occupied - 2) // occupied + 1):
+        column = jnp.sum(jnp.where(lane == low + offset, field, 0.0), axis=1, keepdims=True)
+        spread = jnp.where(walker_ids == low + offset, column, spread)
+    return spread
+
+
+def fused_kernel(
+    n, piece, own_map, trial_ref, trial_own, core_ref, walkers_ref, orbit_own, field_ref, cols_ref,
+    sums_ref, out_ref,
+    blocks, gathered, wide, total, term, right_sems, left_sems, side_sems, recv_sems,
+):
+    rows, occupied = trial_own.shape
+    own = cols_ref.shape[0]
+    points = gathered.shape[0]
+    chips = n // 2
+    far = chips // 2
+    top = (rows // 2 + 15) // 16 * 16
+    parts = ((0, top), (top, rows - top))
+    me = lax.axis_index("pts")
+    core_id = lax.rem(me, 2)
+    chip = me // 2
+    ring = jnp.where(lax.rem(chip, 2) == 0, chip // 2, chips - 1 - chip // 2)
+
+    def device(place, side):
+        place = lax.rem(place + 2 * chips, chips)
+        where = jnp.where(place < far, 2 * place, 2 * (chips - 1 - place) + 1)
+        return 2 * where + side
+
+    right, left, partner = device(ring + 1, core_id), device(ring - 1, core_id), device(ring, 1 - core_id)
+
+    def slot(index, part=None):
+        offset, length = (0, rows) if part is None else parts[part]
+        return gathered.at[pl.ds(pl.multiple_of(index * rows + offset, 16), length), :]
+
+    def send(src, index, part, send_sem, target):
+        return pltpu.make_async_remote_copy(
+            src_ref=src,
+            dst_ref=slot(index, part),
+            send_sem=send_sem,
+            recv_sem=recv_sems.at[index, part or 0],
+            device_id={"pts": target},
+            device_id_type=pl.DeviceIdType.MESH,
+        )
+
+    def forward(index, part, send_sem, target):
+        send(slot(index, part), index, part, send_sem, target).start()
+
+    def arrived(index, part=None):
+        send(slot(index, part), index, part, side_sems.at[0, 0], partner).wait_recv()
+
+    barrier = pltpu.get_barrier_semaphore()
+    for other in (right, left, partner):
+        pl.semaphore_signal(barrier, inc=1, device_id={"pts": other}, device_id_type=pl.DeviceIdType.MESH)
+    pl.semaphore_wait(barrier, 3)
+    send(own_map, me, None, right_sems.at[0], right).start()
+    send(own_map, me, None, left_sems.at[0], left).start()
+    send(own_map, me, None, side_sems.at[0, 0], partner).start()
+    gathered[pl.ds(pl.multiple_of(me * rows, 16), rows), :] = own_map[...]
+    sums_ref[...] = jnp.zeros_like(sums_ref)
+    total[...] = jnp.zeros_like(total)
+    term[...] = cols_ref[...]
+
+    def add_block(index):
+        here = pl.ds(pl.multiple_of(index * rows, 16), rows)
+        block = gathered[here, :]
+        spread = spread_field(field_ref, here, rows, me * own, own, occupied)
+        wide[here, :] = spread
+        current = dot(block, term[...], CONTRACT_LAST).astype(jnp.bfloat16)
+        scaled = (spread * current.astype(jnp.float32)).astype(jnp.bfloat16)
+        total[...] += dot(scaled, block, CONTRACT_FIRST)
+
+    @pl.loop(0, 2 * far + 1)
+    def _(task):
+        hop = task // 2
+        same = lax.rem(task, 2) == 0
+        ahead, behind = device(ring + hop, core_id), device(ring - hop, core_id)
+        ahead_side, behind_side = device(ring + hop, 1 - core_id), device(ring - hop, 1 - core_id)
+        last = hop == far
+        middle = jnp.logical_and(hop > 0, hop < far)
+
+        @pl.when(jnp.logical_and(same, middle))
+        def _():
+            arrived(behind)
+
+            @pl.when(hop < far - 1)
+            def _():
+                forward(behind, None, right_sems.at[hop], right)
+
+            @pl.when(hop == far - 1)
+            def _():
+                forward(behind, 0, right_sems.at[hop], right)
+
+            forward(behind, None, side_sems.at[0, hop], partner)
+            arrived(ahead)
+
+            @pl.when(hop < far - 1)
+            def _():
+                forward(ahead, None, left_sems.at[hop], left)
+
+            @pl.when(hop == far - 1)
+            def _():
+                forward(ahead, 1, left_sems.at[hop], left)
+
+            forward(ahead, None, side_sems.at[1, hop], partner)
+
+        @pl.when(last)
+        def _():
+            for part in range(2):
+                arrived(ahead, part)
+                forward(ahead, part, side_sems.at[part, hop], partner)
+            for part in range(2):
+                arrived(ahead_side, part)
+
+        @pl.when(jnp.logical_not(same))
+        def _():
+            arrived(ahead_side)
+
+            @pl.when(hop > 0)
+            def _():
+                arrived(behind_side)
+
+        near = jnp.where(same, ahead, ahead_side)
+        opposite = jnp.where(last, ahead_side, jnp.where(same, behind, behind_side))
+        pair = jnp.where(jnp.logical_and(last, ring >= far), ahead_side, near)
+        add_exchange(
+            sums_ref, blocks, gathered[pl.ds(pl.multiple_of(pair * rows, 16), rows), :], trial_ref, trial_own,
+            core_ref, walkers_ref, orbit_own, pair * rows, jnp.where(hop == 0, 1.0, 2.0),
+        )
+        add_block(near)
+
+        @pl.when(hop > 0)
+        def _():
+            add_block(opposite)
+
+    running = cols_ref[...].astype(jnp.float32)
+    for degree in range(1, TAYLOR + 1):
+        if degree > 1:
+            total[...] = jnp.zeros_like(total)
+
+            @pl.loop(0, points // piece)
+            def _(number):
+                here = pl.ds(pl.multiple_of(number * piece, piece), piece)
+                block = gathered[here, :]
+                current = dot(block, term[...], CONTRACT_LAST).astype(jnp.bfloat16)
+                scaled = (wide[here, :] * current.astype(jnp.float32)).astype(jnp.bfloat16)
+                total[...] += dot(scaled, block, CONTRACT_FIRST)
+
+        term[...] = (total[...] / degree).astype(jnp.bfloat16)
+        running = running + term[...].astype(jnp.float32)
+    out_ref[...] = running.astype(jnp.bfloat16)
+
+    for hop in range(far):
+        for number, (sems, target) in enumerate(((right_sems, right), (left_sems, left))):
+            part = number if hop == far - 1 and hop > 0 else None
+            send(slot(me, part), me, part, sems.at[hop], target).wait_send()
+    send(slot(me), me, None, side_sems.at[0, 0], partner).wait_send()
+    for hop in range(1, far + 1):
+        for number in range(2):
+            part = number if hop == far else None
+            send(slot(me, part), me, part, side_sems.at[number, hop], partner).wait_send()
+
+
+def fused(n, points_map, trial, trial_here, core, flat_walkers, orbit, field_full, own_cols_t, walker_count):
+    rows, orbitals = points_map.shape
+    points, own, columns = rows * n, own_cols_t.shape[0], flat_walkers.shape[1]
     window = (rows + (LANES - 16) + LANES - 1) // LANES * LANES
-    steps = n // 2 + 1
-    whole = lambda a: pl.BlockSpec(a.shape, lambda s: (0,) * a.ndim)
-    flops = 2 * steps * (rows * orbitals * columns + 2 * rows * window * columns)
+    far = n // 4
+    piece = next(p for p in (1280, 640, 256, rows) if points % p == 0)
+    dma = pltpu.SemaphoreType.DMA
     return pl.pallas_call(
-        functools.partial(exchange_kernel, n, walker_count),
-        grid=(steps,),
-        out_shape=jax.ShapeDtypeStruct((walker_count, 8, window), jnp.float32),
-        in_specs=[
-            pl.BlockSpec((1, rows, orbitals), lambda s: (lax.rem(lax.axis_index("pts") + s, n), 0, 0)),
-            whole(trial),
-            whole(trial_here),
-            whole(core),
-            whole(flat_walkers),
-            whole(orbit),
+        functools.partial(fused_kernel, n, piece),
+        out_shape=(
+            jax.ShapeDtypeStruct((walker_count, 8, window), jnp.float32),
+            jax.ShapeDtypeStruct((own, orbitals), jnp.bfloat16),
+        ),
+        in_specs=[pl.BlockSpec(memory_space=pltpu.VMEM)] * 8,
+        out_specs=[pl.BlockSpec(memory_space=pltpu.VMEM)] * 2,
+        scratch_shapes=[
+            pltpu.VMEM((window, columns), jnp.bfloat16),
+            pltpu.VMEM((points, orbitals), jnp.bfloat16),
+            pltpu.VMEM((points, own), jnp.float32),
+            pltpu.VMEM((own, orbitals), jnp.float32),
+            pltpu.VMEM((own, orbitals), jnp.bfloat16),
+            dma((far,)),
+            dma((far,)),
+            dma((2, far + 1)),
+            dma((n, 2)),
         ],
-        out_specs=pl.BlockSpec((walker_count, 8, window), lambda s: (0, 0, 0)),
-        scratch_shapes=[pltpu.VMEM((window, columns), jnp.bfloat16)],
-        cost_estimate=pl.CostEstimate(flops=flops, bytes_accessed=2 * map_full.size, transcendentals=0),
-        compiler_params=pltpu.CompilerParams(vmem_limit_bytes=60 * 2**20),
-        name="exchange",
-    )(map_full.reshape(n, rows, orbitals), trial, trial_here, core, flat_walkers, orbit)
+        compiler_params=pltpu.CompilerParams(
+            collective_id=0, has_side_effects=True, vmem_limit_bytes=60 * 2**20
+        ),
+        name="fused",
+    )(points_map, trial, trial_here, core, flat_walkers, orbit, field_full, own_cols_t)
 
 
 def propagate_kernel(n, occupied, piece, map_ref, field_ref, cols_ref, out_ref, wide, total, term):
@@ -159,7 +321,6 @@
     walker_count = walkers.shape[1]
     occupied = walkers.shape[2]
     n = lax.axis_size("pts")
-    map_full = lax.all_gather(points_map, "pts", axis=0, tiled=True)
     point_first = lax.axis_index("pts") * point_rows
     trial_here = lax.dynamic_slice_in_dim(trial, point_first, point_rows, 0)
     flat_walkers = walkers.reshape(orbitals, walker_count * occupied)
@@ -180,15 +341,16 @@
     own_cols = walker_count * occupied // n
     col_start = lax.axis_index("pts") * own_cols
     cols_walkers = lax.dynamic_slice_in_dim(flat_walkers, col_start, own_cols, 1)
-    final_t = propagate(n, occupied, map_full, field_full, cols_walkers.T)
+    if point_rows % 16 == 0 and n % 8 == 0:
+        sums, final_t = fused(
+            n, points_map, trial, trial_here, core, flat_walkers, flat_orbit, field_full, cols_walkers.T, walker_count
+        )
+        exchange = jnp.sum(sums, axis=(1, 2))
+    else:
+        map_full = lax.all_gather(points_map, "pts", axis=0, tiled=True)
+        final_t = propagate(n, occupied, map_full, field_full, cols_walkers.T)
+        exchange = exchange_plain(trial, trial_here, core, orbit)
     placed = lax.all_to_all(final_t.T, "pts", split_axis=0, concat_axis=1, tiled=True)
-    if point_rows % 16 == 0 and n % 2 == 0:
-        exchange = jnp.sum(
-            exchange_sums(n, walker_count, map_full, trial, trial_here, core, flat_walkers, flat_orbit),
-            axis=(1, 2),
-        )
-    else:
-        exchange = exchange_plain(trial, trial_here, core, orbit)
     hartree = jnp.sum(density.astype(jnp.float32) * potential, axis=0)
     total_points = point_rows * n
     energy = lax.psum((hartree - exchange / occupied) / (2.0 * total_points), "pts")

time: 234 us -> 202 us (0.86)
  waiting for transfers between devices: 32.8 us -> 0.01 us
  Pallas kernels: 74.3 us -> 93.3 us
  between operations: 14.1 us -> 0.72 us
  blocking collectives: 82.3 us -> 77.2 us
    all_gather x1 -> x0, waiting for transfers between devices: 32.1 us -> none  [body(): map_full = lax.all_gather(points_map, 'pts', axis=0, tiled=True)]
    pallas_call x2 -> x1, Pallas kernels: 74.3 us -> 93.3 us  [fused(): pl.pallas_call(functools.partial(fused_kernel, n, piece), out_shape=(jax....]
    all_gather x1, blocking collectives: 22.1 us -> 19.1 us  [body(): field_full = lax.all_gather(field, 'pts', axis=0, tiled=True)]
  transfers between devices with their start and end apart: 2 -> 1, of which waited for: 1 -> 0; matrix products, arithmetic and copies ran while one was open for 10% -> 1% of each run, Pallas kernels for 18% -> 0%
where the time goes in v2:
time: 202 us
  Pallas kernels  93.3 us (46%)
  blocking collectives  77.2 us (38%)
  local copies, waits for them, and re-layouts  14.8 us (7%)
  matrix products  6.56 us (3%)
  starting transfers between devices  5.35 us (3%)
  other arithmetic  3.63 us (2%)
    pallas_call x1, Pallas kernels, fused(): pl.pallas_call(functools.partial(fused_kernel, n, piece), out_shape=(jax....  93.3 us
    psum x1, blocking collectives, body(): lax.psum((hartree - exchange / occupied) / (2.0 * total_points), 'pts')  34.3 us
    all_gather x1, blocking collectives, body(): lax.all_gather(density, 'pts', axis=0, tiled=True)  23.8 us
    all_gather x1, blocking collectives, body(): field_full = lax.all_gather(field, 'pts', axis=0, tiled=True)  19.1 us
    all_to_all x1, starting transfers between devices, body(): lax.all_to_all(final_t.T, 'pts', split_axis=0, concat_axis=1, tiled=True)  5.35 us
    unnamed x7, local copies, waits for them, and re-layouts  4.26 us
  transfers between devices with their start and end apart: 1, of which 0 were waited for; matrix products, arithmetic and copies ran while one was open for 1% of the time, Pallas kernels for 0%

profile of v2, /device:TPU:0, one launch (start us, length us, event | category | flops | bytes accessed | tf_op | source)
XLA Modules:
  0.0 201.5 jit_solution(15680937901323657675)
XLA Ops:
  0.6 3.2 %copy.17 = bf16[800,12,128]{0,2,1:T(8,128)(2,1)S(1)} copy(bf16[800,12,128]{2,0,1:T(8,128)(2,1)} %param.8) | data formatting | bytes 4915200 | tf_op args[3]
  3.9 0.0 copy-start
  3.9 2.8 %copy.21.walkers_ref = bf16[800,1536]{1,0:T(8,128)(2,1)} copy(bf16[800,1536]{0,1:T(8,128)(2,1)S(1)} %bitcast.21) | data formatting | bytes 4915200 | tf_op jit(solution)/shard_map/reshape | solution.py:326
  6.6 0.7 dynamic-slice_bitcast_fusion.cols_ref
  7.3 0.0 copy-done
  7.3 2.5 %convolution_convert_fusion.orbit_own = bf16[400,1536]{1,0:T(8,128)(2,1)} fusion(bf16[400,800]{1,0:T(8,128)(2,1)S(1)} %copy-done, bf16[800,1536]{0,1:T(8,128)(2,1)S(1)} %bitcast.23), kind=kOutput, calls=%fused_computation.1 | convolution fusion | flops 983654400 | bytes 4326400 | tf_op jit(solution)/shard_map/dot_general | solution.py:327
  9.9 2.5 %reshape.20 = f32[400,12,128]{2,1,0:T(8,128)S(1)} reshape(bf16[400,1536]{1,0:T(8,128)(2,1)} %convolution_convert_fusion.orbit_own) | data formatting | bytes 3686400 | tf_op jit(solution)/shard_map/convert_element_type | solution.py:330
  12.4 0.0 copy-start.1
  12.4 1.6 fusion.1
  13.9 0.9 multiply_reduce_fusion
  14.9 0.1 copy.18
  15.0 23.8 %all-gather = bf16[16,400,12]{1,2,0:T(8,128)(2,1)S(1)} all-gather(bf16[1,400,12]{1,2,0:T(8,128)(2,1)S(1)} %fusion), channel_id=1, replica_groups=mesh['mol'=2,'pts'=16] {'pts'}, dimensions={0}, use_global_device_ids=true | all-gather | bytes 163200 | tf_op jit(solution)/shard_map/all_gather | solution.py:335
  38.8 0.1 copy.19
  38.9 0.3 reshape.22
  39.3 0.0 copy-done.1
  39.3 4.0 %multiply_reduce_fusion.1 = (f32[12]{0:T(128)S(1)}, f32[1,400,12]{1,2,0:T(8,128)S(1)}) fusion(f32[400,12]{0,1:T(8,128)S(1)} %copy.18, s32[400,12]{0,1:T(8,128)S(1)} %copy-done.1, bf16[6400,12]{0,1:T(8,128)(2,1)S(1)} %reshape.22, bf16[400,6400]{1,0:T(8,128)(2,1)} %core_ref.1), kind=kOutput, calls=%fused_computation.4 | convolution fusion | flops 61531188 | bytes 5331248 | tf_op jit(solution)/shard_map/dot_general | solution.py:333
  43.3 19.1 %all-gather.1 = f32[16,400,12]{1,2,0:T(8,128)S(1)} all-gather(f32[1,400,12]{1,2,0:T(8,128)S(1)} %get-tuple-element.13), channel_id=1, replica_groups=mesh['mol'=2,'pts'=16] {'pts'}, dimensions={0}, use_global_device_ids=true | all-gather | bytes 326400 | tf_op jit(solution)/shard_map/all_gather | solution.py:339
  62.4 2.3 %copy.20 = f32[16,400,12]{2,1,0:T(8,128)} copy(f32[16,400,12]{1,2,0:T(8,128)S(1)} %all-gather.1) | data formatting | bytes 614400 | tf_op jit(solution)/shard_map/all_gather | solution.py:339
  64.7 93.3 %fused.1 = (f32[12,8,512]{2,1,0:T(8,128)}, bf16[96,800]{1,0:T(8,128)(2,1)}) custom-call(bf16[400,800]{1,0:T(8,128)(2,1)} %own_map.1, bf16[6400,128]{1,0:T(8,128)(2,1)} %trial_ref.1, bf16[400,128]{1,0:T(8,128)(2,1)} %get-tuple-element.11.trial_own, bf16[400,6400]{1,0:T(8,128)(2,1)} %core_ref.1, bf16[800,1536]{1,0:T(8,128)(2,1)} %copy.21.walkers_ref, ...), custom_call_target="tpu_custom_call" | custom-call | tf_op jit(solution)/shard_map/fused/pallas_call | solution.py:224
  158.0 1.1 copy.22
  159.1 0.7 all_to_all.12
  159.8 5.3 %all-to-all-start = ((bf16[16,50,96]{2,1,0:T(8,128)(2,1)}), bf16[16,50,96]{2,1,0:T(8,128)(2,1)S(1)}, u32[]{:S(2)}, u32[]{:S(2)}) async-start(bf16[16,50,96]{2,1,0:T(8,128)(2,1)} %all_to_all.12), calls=%async_computation | async-start | bytes 458752 | tf_op jit(solution)/shard_map/all_to_all | solution.py:353
  165.2 1.1 reduce_sum.29
  166.3 34.3 %psum.7 = f32[12]{0:T(128)} all-reduce(f32[12]{0:T(128)S(1)} %subtract_multiply_fusion), channel_id=1, replica_groups=mesh['mol'=2,'pts'=16] {'pts'}, use_global_device_ids=true, to_apply=%region_3.4 | all-reduce | flops 12 | bytes 96 | tf_op jit(solution)/shard_map/psum | solution.py:356
  200.6 0.0 all-to-all-done
  200.7 0.2 reshape.19
  200.8 0.7 copy.24
  (3 shorter events, 0.0 us)
Async XLA Ops:
  3.9 3.5 %copy-start = (bf16[400,800]{1,0:T(8,128)(2,1)S(1)}, bf16[400,800]{1,0:T(8,128)(2,1)}, u32[]{:S(2)}) copy-start(bf16[400,800]{1,0:T(8,128)(2,1)} %own_map.1) | copy-start | bytes 1920004
  12.4 26.9 %copy-start.1 = (s32[400,12]{0,1:T(8,128)S(1)}, s32[400,12]{0,1:T(8,128)}, u32[]{:S(2)}) copy-start(s32[400,12]{0,1:T(8,128)} %param.9) | copy-start | bytes 57604
  159.8 40.8 %all-to-all-start = ((bf16[16,50,96]{2,1,0:T(8,128)(2,1)}), bf16[16,50,96]{2,1,0:T(8,128)(2,1)S(1)}, u32[]{:S(2)}, u32[]{:S(2)}) async-start(bf16[16,50,96]{2,1,0:T(8,128)(2,1)} %all_to_all.12), calls=%async_computation | async-start | bytes 458752 | tf_op jit(solution)/shard_map/all_to_all | solution.py:353

commit v3 on v2

--- a/solution.py
+++ b/solution.py
@@ -315,6 +315,12 @@
     return lax.map(per_walker, (jnp.moveaxis(orbit, 1, 0), jnp.moveaxis(everyone, 1, 0)))
 
 
+def gather_stacked(part):
+    n = lax.axis_size("pts")
+    copies = jnp.broadcast_to(part[None], (n,) + part.shape)
+    return lax.all_to_all(copies, "pts", split_axis=0, concat_axis=0, tiled=True)
+
+
 def body(points_map, trial, core, walkers, draws):
     point_rows = points_map.shape[0]
     orbitals = points_map.shape[1]
@@ -332,11 +338,11 @@
     ).astype(jnp.bfloat16)
     potential = jnp.dot(
         core,
-        lax.all_gather(density, "pts", axis=0, tiled=True),
+        jnp.moveaxis(gather_stacked(density.T), 2, 1).reshape(point_rows * n, walker_count),
         preferred_element_type=jnp.float32,
     )
     field = FIELD_STEP * (node_lookup(draws) - FIELD_STEP * potential)
-    field_full = lax.all_gather(field, "pts", axis=0, tiled=True)
+    field_full = jnp.moveaxis(gather_stacked(field.T), 2, 1).reshape(point_rows * n, walker_count)
     own_rows = orbitals // n
     own_cols = walker_count * occupied // n
     col_start = lax.axis_index("pts") * own_cols
@@ -353,7 +359,7 @@
     placed = lax.all_to_all(final_t.T, "pts", split_axis=0, concat_axis=1, tiled=True)
     hartree = jnp.sum(density.astype(jnp.float32) * potential, axis=0)
     total_points = point_rows * n
-    energy = lax.psum((hartree - exchange / occupied) / (2.0 * total_points), "pts")
+    energy = jnp.sum(gather_stacked((hartree - exchange / occupied) / (2.0 * total_points)), axis=0)
     return (placed.reshape(own_rows, walker_count, occupied), energy)
 
 

time: 202 us -> 178 us (0.88)
  blocking collectives: 77.2 us -> 17.2 us
  waiting for transfers between devices: 0.01 us -> 24 us
  starting transfers between devices: 5.35 us -> 13.7 us
  local copies, waits for them, and re-layouts: 14.8 us -> 17.9 us
    all_gather x2 -> x0, blocking collectives: 42.9 us -> none  [the longest x1 23.8 us: body(): lax.all_gather(density, 'pts', axis=0, tiled=True)]
    psum x1 -> x0, blocking collectives: 34.3 us -> none  [body(): lax.psum((hartree - exchange / occupied) / (2.0 * total_points), 'pts')]
    all_to_all x0 -> x1, blocking collectives: none -> 17.2 us  [gather_stacked(): lax.all_to_all(copies, 'pts', split_axis=0, concat_axis=0, tiled=True)]
    all_to_all x0 -> x2, waiting for transfers between devices: none -> 15.1 us  [gather_stacked(): lax.all_to_all(copies, 'pts', split_axis=0, concat_axis=0, tiled=True)]
    all_to_all x0 -> x2, starting transfers between devices: none -> 10.2 us  [gather_stacked(): lax.all_to_all(copies, 'pts', split_axis=0, concat_axis=0, tiled=True)]
    all_to_all x1, waiting for transfers between devices: 0.01 us -> 8.91 us  [body(): lax.all_to_all(final_t.T, 'pts', split_axis=0, concat_axis=1, tiled=True)]
    all_gather x2 -> x0, local copies, waits for them, and re-layouts: 2.42 us -> none  [the longest x1 2.31 us: body(): field_full = lax.all_gather(field, 'pts', axis=0, tiled=True)]
    transpose x0 -> x2, local copies, waits for them, and re-layouts: none -> 2.41 us  [the longest x1 2.3 us: body(): jnp.moveaxis(gather_stacked(field.T), 2, 1)]
  transfers between devices with their start and end apart: 1 -> 3, of which waited for: 0 -> 3; matrix products, arithmetic and copies ran while one was open for 1% -> 3% of each run, Pallas kernels for 0% -> 0%
where the time goes in v3:
time: 178 us
  Pallas kernels  93.3 us (52%)
  waiting for transfers between devices  24 us (13%)
  local copies, waits for them, and re-layouts  17.9 us (10%)
  blocking collectives  17.2 us (10%)
  starting transfers between devices  13.7 us (8%)
  matrix products  6.69 us (4%)
  other arithmetic  4.16 us (2%)
    pallas_call x1, Pallas kernels, fused(): pl.pallas_call(functools.partial(fused_kernel, n, piece), out_shape=(jax....  93.3 us
    all_to_all x1, blocking collectives, gather_stacked(): lax.all_to_all(copies, 'pts', split_axis=0, concat_axis=0, tiled=True)  17.2 us
    all_to_all x2, waiting for transfers between devices, gather_stacked(): lax.all_to_all(copies, 'pts', split_axis=0, concat_axis=0, tiled=True)  15.1 us
    all_to_all x2, starting transfers between devices, gather_stacked(): lax.all_to_all(copies, 'pts', split_axis=0, concat_axis=0, tiled=True)  10.2 us
    all_to_all x1, waiting for transfers between devices, body(): lax.all_to_all(final_t.T, 'pts', split_axis=0, concat_axis=1, tiled=True)  8.91 us
    unnamed x10, local copies, waits for them, and re-layouts  5.56 us
    dot_general x1, matrix products, body(): jnp.dot(core, jnp.moveaxis(gather_stacked(density.T), 2, 1).reshape(point...  4.17 us
  transfers between devices with their start and end apart: 3, of which 3 were waited for; matrix products, arithmetic and copies ran while one was open for 3% of the time, Pallas kernels for 0%

profile of v3, /device:TPU:0, one launch (start us, length us, event | category | flops | bytes accessed | tf_op | source)
XLA Modules:
  0.0 177.8 jit_solution(11797013711300748730)
XLA Ops:
  0.6 0.0 copy-start.2
  0.6 3.3 %copy.41 = bf16[800,12,128]{0,2,1:T(8,128)(2,1)S(1)} copy(bf16[800,12,128]{2,0,1:T(8,128)(2,1)} %param.8) | data formatting | bytes 4915200 | tf_op args[3]
  3.9 0.0 copy-start
  4.0 1.5 copy-done
  5.5 0.0 copy-done.2
  5.5 2.5 %convolution_convert_fusion.orbit_own = bf16[400,1536]{1,0:T(8,128)(2,1)} fusion(bf16[400,800]{1,0:T(8,128)(2,1)S(1)} %copy-done.2, bf16[800,1536]{0,1:T(8,128)(2,1)S(1)} %bitcast.23), kind=kOutput, calls=%fused_computation.1 | convolution fusion | flops 983654400 | bytes 4326400 | tf_op jit(solution)/shard_map/dot_general | solution.py:333
  8.0 2.5 %reshape.43 = f32[400,12,128]{2,1,0:T(8,128)S(1)} reshape(bf16[400,1536]{1,0:T(8,128)(2,1)} %convolution_convert_fusion.orbit_own) | data formatting | bytes 3686400 | tf_op jit(solution)/shard_map/convert_element_type | solution.py:336
  10.5 1.6 fusion.1
  12.1 0.0 copy-start.3
  12.1 0.9 multiply_reduce_fusion
  13.0 0.1 copy.42
  13.2 17.2 %all_to_all.32 = bf16[16,12,400]{2,1,0:T(8,128)(2,1)S(1)} all-to-all(bf16[16,12,400]{2,1,0:T(8,128)(2,1)S(1)} %broadcast_in_dim.44), channel_id=1, replica_groups=mesh['mol'=2,'pts'=16] {'pts'}, dimensions={0} | all-to-all | bytes 307200 | tf_op jit(solution)/shard_map/all_to_all | solution.py:321
  30.4 0.1 copy.43
  30.5 0.3 reshape.40
  30.8 0.0 copy-done.3
  30.9 0.0 copy-start.1
  30.9 4.2 %multiply_reduce_fusion.1 = (f32[12]{0:T(128)S(1)}, f32[12,400]{1,0:T(8,128)S(1)}) fusion(f32[400,12]{0,1:T(8,128)S(1)} %copy.42, s32[400,12]{0,1:T(8,128)S(1)} %copy-done.3, bf16[6400,12]{0,1:T(8,128)(2,1)S(1)} %reshape.40, bf16[400,6400]{1,0:T(8,128)(2,1)} %core_ref.1), kind=kOutput, calls=%fused_computation.4 | convolution fusion | flops 61531188 | bytes 5331248 | tf_op jit(solution)/shard_map/dot_general | solution.py:339
  35.0 0.9 broadcast_in_dim.45
  35.9 3.8 %all-to-all-start.1 = ((f32[16,12,400]{2,1,0:T(8,128)}), f32[16,12,400]{2,1,0:T(8,128)S(1)}, u32[]{:S(2)}, u32[]{:S(2)}) async-start(f32[16,12,400]{2,1,0:T(8,128)} %broadcast_in_dim.45), calls=%async_computation.1 | async-start | bytes 1048576 | tf_op jit(solution)/shard_map/all_to_all | solution.py:321
  39.7 0.0 copy-done.1
  39.7 2.8 %copy.45.walkers_ref = bf16[800,1536]{1,0:T(8,128)(2,1)} copy(bf16[800,1536]{0,1:T(8,128)(2,1)S(1)} %bitcast.24) | data formatting | bytes 4915200 | tf_op jit(solution)/shard_map/reshape | solution.py:332
  42.5 0.7 dynamic-slice_bitcast_fusion.cols_ref
  43.2 10.6 %all-to-all-done.1 = f32[16,12,400]{2,1,0:T(8,128)S(1)} async-done(((f32[16,12,400]{2,1,0:T(8,128)}), f32[16,12,400]{2,1,0:T(8,128)S(1)}, u32[]{:S(2)}, u32[]{:S(2)}) %all-to-all-start.1) | async-done | bytes 307232 | tf_op jit(solution)/shard_map/all_to_all | solution.py:321
  53.7 2.3 %copy.44 = f32[16,400,12]{2,1,0:T(8,128)} copy(f32[16,400,12]{1,2,0:T(8,128)S(1)} %bitcast.26) | data formatting | bytes 614400 | tf_op jit(solution)/shard_map/transpose | solution.py:345
  56.0 93.3 %fused.1 = (f32[12,8,512]{2,1,0:T(8,128)}, bf16[96,800]{1,0:T(8,128)(2,1)}) custom-call(bf16[400,800]{1,0:T(8,128)(2,1)} %own_map.1, bf16[6400,128]{1,0:T(8,128)(2,1)} %trial_ref.1, bf16[400,128]{1,0:T(8,128)(2,1)} %get-tuple-element.17.trial_own, bf16[400,6400]{1,0:T(8,128)(2,1)} %core_ref.1, bf16[800,1536]{1,0:T(8,128)(2,1)} %copy.45.walkers_ref, ...), custom_call_target="tpu_custom_call" | custom-call | tf_op jit(solution)/shard_map/fused/pallas_call | solution.py:224
  149.3 1.1 reduce_sum.38
  150.4 0.6 broadcast_in_dim.46
  151.0 6.5 %all-to-all-start.3 = ((f32[16,1,12]{2,1,0:T(1,128)}), f32[16,1,12]{2,1,0:T(1,128)S(1)}, u32[]{:S(2)}, u32[]{:S(2)}) async-start(f32[16,1,12]{2,1,0:T(1,128)} %broadcast_in_dim.46), calls=%async_computation.3 | async-start | bytes 16384 | tf_op jit(solution)/shard_map/all_to_all | solution.py:321
  157.5 1.1 copy.46
  158.6 0.7 all_to_all.24
  159.3 4.5 %all-to-all-done.3 = f32[16,1,12]{2,1,0:T(1,128)S(1)} async-done(((f32[16,1,12]{2,1,0:T(1,128)}), f32[16,1,12]{2,1,0:T(1,128)S(1)}, u32[]{:S(2)}, u32[]{:S(2)}) %all-to-all-start.3) | async-done | bytes 800 | tf_op jit(solution)/shard_map/all_to_all | solution.py:321
  163.9 3.5 %all-to-all-start.2 = ((bf16[16,50,96]{2,1,0:T(8,128)(2,1)}), bf16[16,50,96]{2,1,0:T(8,128)(2,1)S(1)}, u32[]{:S(2)}, u32[]{:S(2)}) async-start(bf16[16,50,96]{2,1,0:T(8,128)(2,1)} %all_to_all.24), calls=%async_computation.2 | async-start | bytes 458752 | tf_op jit(solution)/shard_map/all_to_all | solution.py:359
  167.4 0.5 reduce_sum.39
  167.9 8.9 %all-to-all-done.2 = bf16[16,50,96]{2,1,0:T(8,128)(2,1)S(1)} async-done(((bf16[16,50,96]{2,1,0:T(8,128)(2,1)}), bf16[16,50,96]{2,1,0:T(8,128)(2,1)S(1)}, u32[]{:S(2)}, u32[]{:S(2)}) %all-to-all-start.2) | async-done | bytes 153632 | tf_op jit(solution)/shard_map/all_to_all | solution.py:359
  176.9 0.2 reshape.42
  177.1 0.7 copy.49
  (4 shorter events, 0.1 us)
Async XLA Ops:
  0.6 4.9 %copy-start.2 = (bf16[400,800]{1,0:T(8,128)(2,1)S(1)}, bf16[400,800]{1,0:T(8,128)(2,1)}, u32[]{:S(2)}) copy-start(bf16[400,800]{1,0:T(8,128)(2,1)} %own_map.1) | copy-start | bytes 1920004
  3.9 1.5 copy-start
  12.1 18.8 %copy-start.3 = (s32[400,12]{0,1:T(8,128)S(1)}, s32[400,12]{0,1:T(8,128)}, u32[]{:S(2)}) copy-start(s32[400,12]{0,1:T(8,128)} %param.9) | copy-start | bytes 57604
  30.9 8.8 %copy-start.1 = (bf16[800,12,128]{0,2,1:T(8,128)(2,1)S(1)}, bf16[800,12,128]{0,2,1:T(8,128)(2,1)}, u32[]{:S(2)}) copy-start(bf16[800,12,128]{0,2,1:T(8,128)(2,1)} %copy-done) | copy-start | bytes 7372804
  35.9 17.8 %all-to-all-start.1 = ((f32[16,12,400]{2,1,0:T(8,128)}), f32[16,12,400]{2,1,0:T(8,128)S(1)}, u32[]{:S(2)}, u32[]{:S(2)}) async-start(f32[16,12,400]{2,1,0:T(8,128)} %broadcast_in_dim.45), calls=%async_computation.1 | async-start | bytes 1048576 | tf_op jit(solution)/shard_map/all_to_all | solution.py:321
  151.0 12.8 %all-to-all-start.3 = ((f32[16,1,12]{2,1,0:T(1,128)}), f32[16,1,12]{2,1,0:T(1,128)S(1)}, u32[]{:S(2)}, u32[]{:S(2)}) async-start(f32[16,1,12]{2,1,0:T(1,128)} %broadcast_in_dim.46), calls=%async_computation.3 | async-start | bytes 16384 | tf_op jit(solution)/shard_map/all_to_all | solution.py:321
  163.9 13.0 %all-to-all-start.2 = ((bf16[16,50,96]{2,1,0:T(8,128)(2,1)}), bf16[16,50,96]{2,1,0:T(8,128)(2,1)S(1)}, u32[]{:S(2)}, u32[]{:S(2)}) async-start(bf16[16,50,96]{2,1,0:T(8,128)(2,1)} %all_to_all.24), calls=%async_computation.2 | async-start | bytes 458752 | tf_op jit(solution)/shard_map/all_to_all | solution.py:359
